TPU v7x, 256 devices: a whole 4x4x8 slice. The times are simulated.
256 devices in a mesh: section: 8 (over y, x_hi), seq: 32 (over z, x_lo, core).
Axes of the slice: x: 4 (x_hi: 2, x_lo: 2; x = x_hi * 2 + x_lo), y: 4, z: 8, core: 2. Of those that a mesh axis runs over, the one named last changes fastest.
Arguments:
- stream: bfloat16 [8, 512, 1536], P('section', 'seq'), may hold values from -6 to 6
- queries: bfloat16 [8, 512, 1536], P('section', 'seq'), may hold values from -40 to 40
- fresh_keys: bfloat16 [8, 512, 1536], P('section', 'seq'), may hold values from -4 to 4
- fresh_values: bfloat16 [8, 512, 1536], P('section', 'seq'), may hold values from -6 to 6
- stale_keys: bfloat16 [8, 4608, 1536], P('section', 'seq'), may hold values from -6 to 6
- stale_values: bfloat16 [8, 4608, 1536], P('section', 'seq'), may hold values from -6 to 6
- gate: float32 [8, 1536], P('section'), may hold values from 0.5 to 4
- patch_of_section: int32 [8], P('section'), may hold values from 0 to 7, as said below
- text_len: int32 [1], replicated, may hold values from 128 to 512
Outputs:
- attended: bfloat16 [8, 512, 1536], P('section', 'seq')
- stream_next: bfloat16 [8, 512, 1536], P('section', 'seq')
Inputs may be any that keep to these rules, and one draw needn't show every extreme that they name: `patch_of_section`: section s works on patch (c - s) mod 8 for one c of the draw. The first text_len text positions are used.
All inputs are finite; a program needn't handle non-finite values.
Results may differ from a plain program's by a relative error of at most 0.0085.
Values may be sent and summed in bfloat16 or wider, within the bound.
A program may use at most 64 MiB of HBM per device.

v0:
```python
import math

import jax
import jax.numpy as jnp
from jax import lax
from jax.sharding import PartitionSpec as P

HEADS = 12
HDIM = 128
TXT = 512


FLOOR_SCORE = -1e30


def passed_along(value, axis, steps):
    count = lax.axis_size(axis)
    pairs = [(source, (source + steps) % count) for source in range(count)]
    return lax.ppermute(value, axis, pairs)


def laid_out(pieces, dim):
    pieces = jnp.moveaxis(pieces, 0, dim)
    dims = pieces.shape
    return pieces.reshape(*dims[:dim], dims[dim] * dims[dim + 1], *dims[dim + 2 :])


def from_everyone(shard, axis):
    copies = jnp.broadcast_to(shard, (lax.axis_size(axis), *shard.shape))
    return lax.all_to_all(copies, axis, split_axis=0, concat_axis=0, tiled=True)


def gather_directly(shard, axis, dim):
    return laid_out(from_everyone(shard, axis), dim)


def over_copies(shard, axis):
    return from_everyone(shard, axis).max(axis=0)


def side_by_side(arrays, axis, dim, along):
    widths = [a.shape[along] for a in arrays]
    both = jnp.concatenate(arrays, axis=along)
    result = lax.psum_scatter(both, axis, scatter_dimension=dim, tiled=True)
    return tuple(jnp.split(result, [sum(widths[:k]) for k in range(1, len(widths))], axis=along))


def head_scores(query_rows, key_rows):
    query_heads = query_rows.reshape(query_rows.shape[0], HEADS, HDIM)
    key_heads = key_rows.reshape(key_rows.shape[0], HEADS, HDIM)
    return jnp.einsum(
        "qhd,khd->hqk", query_heads, key_heads, preferred_element_type=jnp.float32
    ) / math.sqrt(HDIM)


def weighted_values(weights, value_rows):
    value_heads = value_rows.reshape(value_rows.shape[0], HEADS, HDIM)
    return jnp.einsum(
        "hqk,khd->qhd",
        weights.astype(jnp.bfloat16),
        value_heads,
        preferred_element_type=jnp.float32,
    )


def stale_allowed(first_row, piece_rows, patch_index, text_count, patch_length):
    positions = first_row + jnp.arange(piece_rows, dtype=jnp.int32)
    region = (positions - TXT) // patch_length
    return jnp.where(positions < TXT, positions < text_count, region != patch_index)


def local(
    stream,
    queries,
    fresh_keys,
    fresh_values,
    stale_keys,
    stale_values,
    gate,
    patch_of_section,
    text_len,
):
    incoming = passed_along(stream, "section", 1)
    row_count = queries.shape[1]
    patch_length = row_count * lax.axis_size("seq")
    patch_index = patch_of_section[0]
    text_count = text_len[0]
    everyone = gather_directly(queries, "seq", 1)[0]
    stale_rows = stale_keys.shape[1]
    key_rows = jnp.concatenate([stale_keys[0], fresh_keys[0]], 0)
    value_rows = jnp.concatenate([stale_values[0], fresh_values[0]], 0)
    first_row = lax.axis_index("seq") * stale_rows
    allowed = jnp.concatenate(
        [
            stale_allowed(first_row, stale_rows, patch_index, text_count, patch_length),
            jnp.ones((row_count,), dtype=bool),
        ],
        0,
    )
    scores = jnp.where(allowed[None, None, :], head_scores(everyone, key_rows), FLOOR_SCORE)
    local_max = jnp.max(scores, axis=2)
    global_max = over_copies(local_max, "seq")
    weights = jnp.where(allowed[None, None, :], jnp.exp(scores - local_max[:, :, None]), 0.0)
    factor = jnp.exp(local_max - global_max)
    partial_value = weighted_values(weights, value_rows) * jnp.transpose(factor)[:, :, None]
    partial_value = partial_value.reshape(patch_length, HEADS * HDIM)
    weight_sums = jnp.transpose(jnp.sum(weights, axis=2) * factor)
    weighted, row_sums = side_by_side((partial_value, weight_sums), "seq", 0, 1)
    averaged = weighted.reshape(row_count, HEADS, HDIM) / row_sums[:, :, None]
    attended = averaged.reshape(1, row_count, HEADS * HDIM).astype(jnp.bfloat16)
    stream_next = (
        incoming.astype(jnp.float32) + gate[:, None, :] * attended.astype(jnp.float32)
    ).astype(jnp.bfloat16)
    return (attended, stream_next)


def solution(mesh):
    placed = (
        P("section", "seq", None),
        P("section", "seq", None),
        P("section", "seq", None),
        P("section", "seq", None),
        P("section", "seq", None),
        P("section", "seq", None),
        P("section", None),
        P("section"),
        P(),
    )
    return jax.shard_map(
        local,
        mesh=mesh,
        in_specs=placed,
        out_specs=(P("section", "seq", None), P("section", "seq", None)),
        check_vma=False,
    )
```

profile of v0, /device:TPU:1, one launch (start us, length us, event | category | flops | bytes accessed | tf_op | source)
XLA Modules:
  0.0 235.3 jit_solution(9674692152763349219)
XLA Ops:
  7.2 0.0 copy-start
  7.2 0.0 copy-start.2
  7.2 2.2 broadcast_in_dim.34
  9.4 11.0 %all-to-all-start = ((bf16[32,1,16,1536]{3,2,1,0:T(8,128)(2,1)}), bf16[32,1,16,1536]{3,2,1,0:T(8,128)(2,1)S(1)}, u32[]{:S(2)}, u32[]{:S(2)}) async-start(bf16[32,1,16,1536]{3,2,1,0:T(8,128)(2,1)} %broadcast_in_dim.34), calls=%async_computation | async-start | bytes 3145728 | tf_op jit(solution)/shard_map/all_to_all | solution.py:30
  21.7 0.0 copy-done
  21.7 0.3 concatenate.26
  22.1 0.1 copy.40
  22.2 0.0 copy-done.2
  22.2 0.1 concatenate.27
  22.3 37.3 %all-to-all-done = bf16[32,1,16,1536]{3,2,1,0:T(8,128)(2,1)S(1)} async-done(((bf16[32,1,16,1536]{3,2,1,0:T(8,128)(2,1)}), bf16[32,1,16,1536]{3,2,1,0:T(8,128)(2,1)S(1)}, u32[]{:S(2)}, u32[]{:S(2)}) %all-to-all-start) | async-done | bytes 1572896 | tf_op jit(solution)/shard_map/all_to_all | solution.py:30
  59.6 2.1 reshape_squeeze_reshape_transpose.3
  61.7 0.0 copy-start.1
  61.7 4.8 %bitcast_reduce_fusion = (f32[12,512]{1,0:T(8,128)S(1)}, f32[12,160,512]{2,1,0:T(8,128)}) fusion(pred[160]{0:T(512)(128)(4,1)S(1)} %concatenate.25, bf16[512,12,128]{2,1,0:T(8,128)(2,1)} %reshape_squeeze_reshape_transpose.3, bf16[16,12,128]{2,0,1:T(8,128)(2,1)S(1)} %copy.41, bf16[144,12,128]{2,0,1:T(8,128)(2,1)S(1)} %copy.40), kind=kOutput, calls=%fused_computation.1 | convolution fusion | flops 255584256 | bytes 6021280 | tf_op jit(solution)/shard_map/qhd,khd->hqk/dot_general | solution.py:51
  66.5 0.0 copy-start.3
  66.5 1.1 broadcast_in_dim.37
  67.6 4.5 %all-to-all-start.1 = ((f32[32,12,512]{2,1,0:T(8,128)}), f32[32,12,512]{2,1,0:T(8,128)S(1)}, u32[]{:S(2)}, u32[]{:S(2)}) async-start(f32[32,12,512]{2,1,0:T(8,128)} %broadcast_in_dim.37), calls=%async_computation.1 | async-start | bytes 2097152 | tf_op jit(solution)/shard_map/all_to_all | solution.py:30
  72.0 0.0 reduce-scatter.2.cloned.1.call-start
  72.1 0.0 copy-done.1
  72.1 0.3 concatenate.22
  72.4 0.1 copy.38
  72.6 0.0 copy-done.3
  72.6 0.1 concatenate.23
  72.6 3.2 %fusion.2 = f32[12,512]{1,0:T(8,128)S(1)} fusion(f32[12,160,512]{2,1,0:T(8,128)} %get-tuple-element.7, f32[12,512]{1,0:T(8,128)S(1)} %get-tuple-element.6, pred[160]{0:T(512)(128)(4,1)S(1)} %concatenate.25), kind=kLoop, calls=%fused_computation.7 | loop fusion | flops 4909056 | bytes 3981472 | tf_op jit(solution)/shard_map/reduce_sum | solution.py:107
  75.8 24.3 %all-to-all-done.1 = f32[32,12,512]{2,1,0:T(8,128)S(1)} async-done(((f32[32,12,512]{2,1,0:T(8,128)}), f32[32,12,512]{2,1,0:T(8,128)S(1)}, u32[]{:S(2)}, u32[]{:S(2)}) %all-to-all-start.1) | async-done | bytes 786464 | tf_op jit(solution)/shard_map/all_to_all | solution.py:30
  100.1 0.1 reduce_max.19
  100.2 5.1 %bitcast_multiply_fusion = f32[512,12,128]{0,2,1:T(8,128)} fusion(f32[12,160,512]{2,1,0:T(8,128)} %get-tuple-element.7, f32[12,512]{1,0:T(8,128)S(1)} %get-tuple-element.6, pred[160]{0:T(512)(128)(4,1)S(1)} %concatenate.25, f32[512,12]{0,1:T(8,128)S(1)} %get-tuple-element.5, bf16[16,12,128]{2,0,1:T(8,128)(2,1)S(1)} %copy.39, bf16[144,12,128]{2,0,1:T(8,128)(2,1)S(1)} %copy.38), kind=kOutput, calls=%fused_computation.6 | convolution fusion | flops 258342912 | bytes 7618720 | tf_op jit(solution)/shard_map/hqk,khd->qhd/dot_general | solution.py:58
  105.3 2.4 %copy.44 = f32[512,1536]{1,0:T(8,128)S(1)} copy(f32[512,1536]{0,1:T(8,128)} %bitcast.40) | data formatting | bytes 6291456 | tf_op jit(solution)/shard_map/reshape | solution.py:106
  107.7 0.1 copy.45
  107.8 0.0 copy-start.5
  107.9 0.0 copy-start.4
  107.9 1.9 pad_maximum_fusion
  109.8 0.0 reduce-scatter.2.cloned.1.call-update
  109.8 0.0 copy-done.5
  109.9 2.5 %collective-permute-start = (bf16[1,16,1536]{2,1,0:T(8,128)(2,1)S(1)}, bf16[1,16,1536]{2,1,0:T(8,128)(2,1)S(1)}, u32[]{:S(2)}, u32[]{:S(2)}) collective-permute-start(bf16[1,16,1536]{2,1,0:T(8,128)(2,1)S(1)} %copy-done.5), channel_id=1, source_target_pairs={{0,32},{32,64},{64,96},{96,128},{128,160},{160,192},{192,224},{224... | collective-permute-start | bytes 147464 | tf_op jit(solution)/shard_map/ppermute | solution.py:19
  112.4 0.0 copy-done.4
  112.4 113.7 %reduce-scatter.2.cloned.1.call-done = f32[16,1548]{1,0:T(8,128)} async-done(((f32[512,1548]{1,0:T(8,128)}), f32[16,1548]{1,0:T(8,128)}) %reduce-scatter.2.cloned.1.call-update) | async-done | bytes 99088 | tf_op jit(solution)/shard_map/reduce_scatter | solution.py:44
  226.1 0.7 split.9
  226.8 0.0 collective-permute-done
  226.8 0.1 div.35
  226.9 1.6 fusion.23
  (6 shorter events, 0.1 us)
Async XLA Ops:
  7.2 14.6 %copy-start = (bf16[1,144,1536]{2,1,0:T(8,128)(2,1)S(1)}, bf16[1,144,1536]{2,1,0:T(8,128)(2,1)}, u32[]{:S(2)}) copy-start(bf16[1,144,1536]{2,1,0:T(8,128)(2,1)} %param.13) | copy-start | bytes 1327108
  7.2 15.0 %copy-start.2 = (bf16[1,16,1536]{2,1,0:T(8,128)(2,1)S(1)}, bf16[1,16,1536]{2,1,0:T(8,128)(2,1)}, u32[]{:S(2)}) copy-start(bf16[1,16,1536]{2,1,0:T(8,128)(2,1)} %param.11) | copy-start | bytes 147460
  9.4 50.2 %all-to-all-start = ((bf16[32,1,16,1536]{3,2,1,0:T(8,128)(2,1)}), bf16[32,1,16,1536]{3,2,1,0:T(8,128)(2,1)S(1)}, u32[]{:S(2)}, u32[]{:S(2)}) async-start(bf16[32,1,16,1536]{3,2,1,0:T(8,128)(2,1)} %broadcast_in_dim.34), calls=%async_computation | async-start | bytes 3145728 | tf_op jit(solution)/shard_map/all_to_all | solution.py:30
  61.7 10.4 %copy-start.1 = (bf16[1,144,1536]{2,1,0:T(8,128)(2,1)S(1)}, bf16[1,144,1536]{2,1,0:T(8,128)(2,1)}, u32[]{:S(2)}) copy-start(bf16[1,144,1536]{2,1,0:T(8,128)(2,1)} %param.14) | copy-start | bytes 1327108
  66.5 6.1 %copy-start.3 = (bf16[1,16,1536]{2,1,0:T(8,128)(2,1)S(1)}, bf16[1,16,1536]{2,1,0:T(8,128)(2,1)}, u32[]{:S(2)}) copy-start(bf16[1,16,1536]{2,1,0:T(8,128)(2,1)} %param.12) | copy-start | bytes 147460
  67.6 32.5 %all-to-all-start.1 = ((f32[32,12,512]{2,1,0:T(8,128)}), f32[32,12,512]{2,1,0:T(8,128)S(1)}, u32[]{:S(2)}, u32[]{:S(2)}) async-start(f32[32,12,512]{2,1,0:T(8,128)} %broadcast_in_dim.37), calls=%async_computation.1 | async-start | bytes 2097152 | tf_op jit(solution)/shard_map/all_to_all | solution.py:30
  72.0 154.0 %reduce-scatter.2.cloned.1.call-start = ((), (), s32[]{:S(2)}) async-start(), calls=%async_computation.3 | async-start | bytes 3514368 | tf_op jit(solution)/shard_map/reduce_scatter | solution.py:44
  107.8 2.0 copy-start.5
  107.9 4.5 %copy-start.4 = (f32[1,1536]{1,0:T(1,128)S(1)}, f32[1,1536]{1,0:T(1,128)}, u32[]{:S(2)}) copy-start(f32[1,1536]{1,0:T(1,128)} %param.15) | copy-start | bytes 18436
  109.9 116.9 %collective-permute-start = (bf16[1,16,1536]{2,1,0:T(8,128)(2,1)S(1)}, bf16[1,16,1536]{2,1,0:T(8,128)(2,1)S(1)}, u32[]{:S(2)}, u32[]{:S(2)}) collective-permute-start(bf16[1,16,1536]{2,1,0:T(8,128)(2,1)S(1)} %copy-done.5), channel_id=1, source_target_pairs={{0,32},{32,64},{64,96},{96,128},{128,160},{160,192},{192,224},{224... | collective-permute-start | bytes 147464 | tf_op jit(solution)/shard_map/ppermute | solution.py:19
Sparse Core Ops, SparseCore 0:
  110.0 116.0 reduce-scatter.1
where the time goes:
time: 239 us; the launch traced here: 235 us
  waiting for transfers between devices  175 us (73%)
  starting transfers between devices  18.1 us (8%)
  between operations  15.5 us (6%)
  matrix products  9.87 us (4%)
  local copies, waits for them, and re-layouts  9.72 us (4%)
  other arithmetic  6.85 us (3%)
    reduce_scatter x1, waiting for transfers between devices, side_by_side(): result = lax.psum_scatter(both, axis, scatter_dimension=dim, tiled=True)  114 us
    all_to_all x2, waiting for transfers between devices, from_everyone(): return lax.all_to_all(copies, axis, split_axis=0, concat_axis=0, tiled=True)  61.6 us
    all_to_all x2, starting transfers between devices, from_everyone(): return lax.all_to_all(copies, axis, split_axis=0, concat_axis=0, tiled=True)  15.5 us
    dot_general x1, matrix products, weighted_values(): jnp.einsum('hqk,khd->qhd', weights.astype(jnp.bfloat16), value_heads, pre...  5.09 us
  transfers between devices with their start and end apart: 4, of which 3 were waited for; matrix products, arithmetic and copies ran while one was open for 2% of the time, Pallas kernels for 0%

commit v1 on v0

v1 whole, which is shorter than its diff:
```python
import functools
import math

import jax
import jax.numpy as jnp
from jax import lax
from jax.experimental import pallas as pl
from jax.experimental.pallas import tpu as pltpu
from jax.sharding import PartitionSpec as P

HEADS = 12
HDIM = 128
TXT = 512
QUAD = 4
FLOOR_SCORE = -1e30
SCALE = math.log2(math.e) / math.sqrt(HDIM)
MESH = pl.DeviceIdType.MESH


def kernel(
    zs,
    sections,
    stream,
    queries,
    fresh_k,
    fresh_v,
    stale_k,
    stale_v,
    gate,
    patch,
    text,
    att_out,
    next_out,
    q_all,
    k_all,
    v_all,
    part,
    stat,
    got,
    got_stat,
    fin,
    rows_in,
    incoming,
    gate_v,
    next_v,
    local_sem,
    stream_sem,
    q_send,
    q_recv,
    kv_send,
    kv_recv,
    zq_send,
    zq_recv,
    p_send,
    p_recv,
    s_send,
    s_recv,
    f_send,
    f_recv,
):
    section = lax.axis_index("section")
    rank = lax.axis_index("seq")
    z = rank // QUAD
    g = rank % QUAD
    stale = stale_k.shape[0]
    rows = queries.shape[0]
    width = queries.shape[1] // QUAD
    block = rows * QUAD
    heads = width // HDIM

    def quad_peer(k):
        return (g + k) % QUAD

    def z_peer(d):
        return ((z + d) % zs) * QUAD + g

    barrier = pltpu.get_barrier_semaphore()
    peers = [{"seq": z * QUAD + quad_peer(k)} for k in range(1, QUAD)]
    peers += [{"seq": z_peer(d)} for d in range(1, zs)]
    peers += [{"section": (section + 1) % sections}, {"section": (section + sections - 1) % sections}]
    for peer in peers:
        pl.semaphore_signal(barrier, inc=1, device_id=peer, device_id_type=MESH)

    def columns(group):
        return pl.ds(pl.multiple_of(group * width, 128), width)

    def quad_rows(group, count, first=0):
        return pl.ds(pl.multiple_of(first + group * count, 16), count)

    stale_total = stale * QUAD
    sources = (
        (stale_k, k_all, quad_rows(g, stale)),
        (fresh_k, k_all, quad_rows(g, rows, stale_total)),
        (stale_v, v_all, quad_rows(g, stale)),
        (fresh_v, v_all, quad_rows(g, rows, stale_total)),
    )
    mine = columns(g)
    local = [
        pltpu.make_async_copy(queries.at[:, mine], q_all.at[0, quad_rows(g, rows)], local_sem.at[0])
    ]
    for n, (src, dst, where) in enumerate(sources):
        local.append(pltpu.make_async_copy(src.at[:, mine], dst.at[where], local_sem.at[1 + n]))
    local.append(pltpu.make_async_copy(gate, gate_v, local_sem.at[5]))
    for copy in local:
        copy.start()

    pl.semaphore_wait(barrier, len(peers))

    def remote(src, dst, send, recv, peer):
        return pltpu.make_async_remote_copy(
            src_ref=src, dst_ref=dst, send_sem=send, recv_sem=recv, device_id=peer, device_id_type=MESH
        )

    quad_q = []
    for k in range(1, QUAD):
        copy = remote(
            queries.at[:, columns(quad_peer(k))],
            q_all.at[0, quad_rows(g, rows)],
            q_send.at[k - 1],
            q_recv.at[k - 1],
            {"seq": z * QUAD + quad_peer(k)},
        )
        copy.start()
        quad_q.append(copy)
    quad_kv = []
    for n, (src, dst, where) in enumerate(sources):
        for k in range(1, QUAD):
            copy = remote(
                src.at[:, columns(quad_peer(k))],
                dst.at[where],
                kv_send.at[n, k - 1],
                kv_recv.at[n, k - 1],
                {"seq": z * QUAD + quad_peer(k)},
            )
            copy.start()
            quad_kv.append(copy)
    stream_copy = remote(
        stream, incoming, stream_sem.at[0], stream_sem.at[1], {"section": (section + 1) % sections}
    )
    stream_copy.start()

    local[0].wait()
    for copy in quad_q:
        copy.wait_recv()
    order = [d for pair in zip(range(zs // 2, 0, -1), range(zs // 2, zs)) for d in pair]
    order = [d for n, d in enumerate(order) if d not in order[:n]]
    z_q = {}
    for d in order:
        copy = remote(q_all.at[0], q_all.at[d], zq_send.at[d], zq_recv.at[d], {"seq": z_peer(d)})
        copy.start()
        z_q[d] = copy

    spot = lax.broadcasted_iota(jnp.int32, (1, stale_total + block), 1)
    position = z * stale_total + spot
    patch_rows = block * zs
    region = (position - TXT) // patch_rows
    floor = jnp.float32(FLOOR_SCORE)
    text_bias = jnp.where(position < text[0], 0.0, floor)
    image_bias = jnp.where(region == patch[0], floor, 0.0)
    bias = jnp.where(position < TXT, text_bias, image_bias)
    bias = jnp.where(spot < stale_total, bias, 0.0)

    for copy in local[1:]:
        copy.wait()
    for copy in quad_kv:
        copy.wait_recv()

    lane = lax.broadcasted_iota(jnp.int32, (block, 128), 1)
    sent = []
    for d in [0] + order[::-1]:
        if d:
            z_q[d].wait_recv()
        o_ref = got.at[0] if d == 0 else part.at[d]
        s_ref = got_stat.at[0] if d == 0 else stat.at[d]
        stats = jnp.zeros((block, 128), jnp.float32)
        for h in range(heads):
            cols = slice(h * HDIM, (h + 1) * HDIM)
            s = lax.dot_general(
                q_all[d, :, cols],
                k_all[:, cols],
                (((1,), (1,)), ((), ())),
                preferred_element_type=jnp.float32,
            )
            s = s * SCALE + bias
            m = jnp.max(s, axis=1, keepdims=True)
            p = jnp.exp2(s - m)
            total = jnp.sum(p, axis=1, keepdims=True)
            o = jnp.dot(p.astype(jnp.bfloat16), v_all[:, cols], preferred_element_type=jnp.float32)
            o_ref[:, cols] = o.astype(jnp.bfloat16)
            stats = jnp.where(lane == h, m, stats)
            stats = jnp.where(lane == heads + h, total, stats)
        s_ref[:, 0:block] = jnp.transpose(stats)[0:8, :]
        if d:
            peer = {"seq": z_peer(zs - d)}
            for src, dst, send, recv in ((part, got, p_send, p_recv), (stat, got_stat, s_send, s_recv)):
                copy = remote(src.at[d], dst.at[d], send.at[d], recv.at[d], peer)
                copy.start()
                sent.append(copy)

    for copy in sent:
        copy.wait_recv()
    tops = [got_stat[d, 0:heads, 0:block] for d in range(zs)]
    sums = [got_stat[d, heads : 2 * heads, 0:block] for d in range(zs)]
    best = functools.reduce(jnp.maximum, tops)
    factors = [jnp.exp2(t - best) for t in tops]
    whole = functools.reduce(jnp.add, [f * s for f, s in zip(factors, sums)])
    inverse = 1.0 / whole
    rowed = jnp.concatenate([f * inverse for f in factors], axis=0)
    pad = jnp.zeros((128 - heads * zs, block), jnp.float32)
    weight = jnp.transpose(jnp.concatenate([rowed, pad], axis=0))
    for h in range(heads):
        cols = slice(h * HDIM, (h + 1) * HDIM)
        acc = jnp.zeros((block, HDIM), jnp.float32)
        for d in range(zs):
            n = d * heads + h
            acc = acc + weight[:, n : n + 1] * got[d, :, cols].astype(jnp.float32)
        fin[:, cols] = acc.astype(jnp.bfloat16)

    out = []
    for k in range(1, QUAD):
        copy = remote(
            fin.at[quad_rows(quad_peer(k), rows)],
            rows_in.at[g],
            f_send.at[k - 1],
            f_recv.at[k - 1],
            {"seq": z * QUAD + quad_peer(k)},
        )
        copy.start()
        out.append(copy)
    rows_in[g] = fin[quad_rows(g, rows), :]
    stream_copy.wait_recv()
    for copy in out:
        copy.wait_recv()
    for k in range(QUAD):
        cols = slice(k * width, (k + 1) * width)
        att = rows_in[k]
        att_out[:, cols] = att
        next_out[:, cols] = (
            incoming[:, cols].astype(jnp.float32) + gate_v[:, cols] * att.astype(jnp.float32)
        ).astype(jnp.bfloat16)
    for copy in quad_q + quad_kv + [stream_copy] + list(z_q.values()) + sent + out:
        copy.wait_send()


def local(mesh_sizes, stream, queries, fresh_keys, fresh_values, stale_keys, stale_values, gate, patch, text):
    sections, seq = mesh_sizes
    zs = seq // QUAD
    rows, channels = queries.shape[1:]
    stale = stale_keys.shape[1]
    width = channels // QUAD
    block = rows * QUAD
    keys = (stale + rows) * QUAD
    bf16, f32 = jnp.bfloat16, jnp.float32
    dma = pltpu.SemaphoreType.DMA
    hbm = pl.BlockSpec(memory_space=pl.ANY)
    smem = pl.BlockSpec(memory_space=pltpu.SMEM)
    vmem = pl.BlockSpec(memory_space=pltpu.VMEM)
    att, nxt = pl.pallas_call(
        functools.partial(kernel, zs, sections),
        out_shape=[jax.ShapeDtypeStruct((rows, channels), bf16)] * 2,
        in_specs=[hbm] * 7 + [smem] * 2,
        out_specs=[vmem] * 2,
        scratch_shapes=[
            pltpu.VMEM((zs, block, width), bf16),
            pltpu.VMEM((keys, width), bf16),
            pltpu.VMEM((keys, width), bf16),
            pltpu.VMEM((zs, block, width), bf16),
            pltpu.VMEM((zs, 8, 128), f32),
            pltpu.VMEM((zs, block, width), bf16),
            pltpu.VMEM((zs, 8, 128), f32),
            pltpu.VMEM((block, width), bf16),
            pltpu.VMEM((QUAD, rows, width), bf16),
            pltpu.VMEM((rows, channels), bf16),
            pltpu.VMEM((1, channels), f32),
            pltpu.VMEM((rows, channels), bf16),
            dma((6,)),
            dma((2,)),
            dma((3,)),
            dma((3,)),
            dma((4, 3)),
            dma((4, 3)),
            dma((zs,)),
            dma((zs,)),
            dma((zs,)),
            dma((zs,)),
            dma((zs,)),
            dma((zs,)),
            dma((3,)),
            dma((3,)),
        ],
        compiler_params=pltpu.CompilerParams(collective_id=0, has_side_effects=True),
    )(
        stream[0],
        queries[0],
        fresh_keys[0],
        fresh_values[0],
        stale_keys[0],
        stale_values[0],
        gate,
        patch,
        text,
    )
    return att[None], nxt[None]


def solution(mesh):
    rowed = P("section", "seq", None)
    return jax.shard_map(
        functools.partial(local, (mesh.shape["section"], mesh.shape["seq"])),
        mesh=mesh,
        in_specs=(rowed,) * 6 + (P("section", None), P("section"), P()),
        out_specs=(rowed, rowed),
        check_vma=False,
    )
```

time: 239 us -> 49.8 us (0.21); the launches traced: 235 us -> 49.7 us
  waiting for transfers between devices: 175 us -> 0 us
  Pallas kernels: 0 us -> 45.7 us
  starting transfers between devices: 18.1 us -> 0 us
  between operations: 15.5 us -> 1.94 us
  matrix products: 9.87 us -> 0 us
  local copies, waits for them, and re-layouts: 9.72 us -> 2.06 us
  other arithmetic: 6.85 us -> 0 us
    reduce_scatter x1 -> x0, waiting for transfers between devices: 114 us -> none  [side_by_side(): result = lax.psum_scatter(both, axis, scatter_dimension=dim, tiled=True)]
    all_to_all x2 -> x0, waiting for transfers between devices: 61.6 us -> none  [from_everyone(): return lax.all_to_all(copies, axis, split_axis=0, concat_axis=0, tiled=True)]
    pallas_call x0 -> x1, Pallas kernels: none -> 45.7 us  [local(): pl.pallas_call(functools.partial(kernel, zs, sections), out_shape=[jax.Sh...]
    all_to_all x2 -> x0, starting transfers between devices: 15.5 us -> none  [from_everyone(): return lax.all_to_all(copies, axis, split_axis=0, concat_axis=0, tiled=True)]
    dot_general x2 -> x0, matrix products: 9.87 us -> none  [the longest x1 5.09 us: weighted_values(): jnp.einsum('hqk,khd->qhd', weights.astype(jnp.bfloat16), value_heads, pre...]
    broadcast_in_dim x2 -> x0, local copies, waits for them, and re-layouts: 3.31 us -> none  [from_everyone(): copies = jnp.broadcast_to(shard, (lax.axis_size(axis), *shard.shape))]
    reduce_sum x1 -> x0, other arithmetic: 3.19 us -> none  [local(): weight_sums = jnp.transpose(jnp.sum(weights, axis=2) * factor)]
    ppermute x1 -> x0, starting transfers between devices: 2.54 us -> none  [passed_along(): return lax.ppermute(value, axis, pairs)]
  transfers between devices with their start and end apart: 4 -> 0, of which waited for: 3 -> 0; matrix products, arithmetic and copies ran while one was open for 2% -> 0% of each run, Pallas kernels for 0% -> 0%
where the time goes in v1:
time: 49.8 us; the launch traced here: 49.7 us
  Pallas kernels  45.7 us (92%)
  local copies, waits for them, and re-layouts  2.06 us (4%)
  between operations  1.94 us (4%)
    pallas_call x1, Pallas kernels, local(): pl.pallas_call(functools.partial(kernel, zs, sections), out_shape=[jax.Sh...  45.7 us
    unnamed x4, local copies, waits for them, and re-layouts  2.06 us

profile of v1, /device:TPU:1, one launch (start us, length us, event | category | flops | bytes accessed | tf_op | source)
XLA Modules:
  0.0 49.7 jit_solution(4616306251676167776)
XLA Ops:
  1.9 45.7 %shard_map.104 = (bf16[16,1536]{1,0:T(8,128)(2,1)}, bf16[16,1536]{1,0:T(8,128)(2,1)}) custom-call(bf16[16,1536]{1,0:T(8,128)(2,1)} %bitcast.10, bf16[16,1536]{1,0:T(8,128)(2,1)} %bitcast.11, bf16[16,1536]{1,0:T(8,128)(2,1)} %bitcast.12, bf16[16,1536]{1,0:T(8,128)(2,1)} %bitcast.13, bf16[144,1536]{1,0:T(8,128)(2,1)} %bitcast.8, bf16[144,1536]{1,0:T(8,128)(2,1)} %bitcast.9, ...), custom_call_target="tpu_custom_call" | custom-call | tf_op jit(solution)/shard_map/pallas_call | solution.py:258
  47.6 0.0 copy-start
  47.6 1.4 %copy.15 = bf16[1,16,1536]{2,1,0:T(8,128)(2,1)} copy(bf16[1,16,1536]{2,1,0:T(8,128)(2,1)} %bitcast.15) | data formatting | bytes 98304
  49.0 0.0 copy-done
  49.1 0.6 %copy.16 = bf16[1,16,1536]{2,1,0:T(8,128)(2,1)} copy(bf16[1,16,1536]{2,1,0:T(8,128)(2,1)S(1)} %bitcast.14) | data formatting | bytes 98304
Async XLA Ops:
  47.6 1.4 %copy-start = (bf16[16,1536]{1,0:T(8,128)(2,1)S(1)}, bf16[16,1536]{1,0:T(8,128)(2,1)}, u32[]{:S(2)}) copy-start(bf16[16,1536]{1,0:T(8,128)(2,1)} %get-tuple-element.5) | copy-start | bytes 147460

commit v2 on v1

v2 whole, which is shorter than its diff:
```python
import functools
import math

import jax
import jax.numpy as jnp
from jax import lax
from jax.experimental import pallas as pl
from jax.experimental.pallas import tpu as pltpu
from jax.sharding import PartitionSpec as P

HDIM = 128
TXT = 512
QUAD = 4
FLOOR_SCORE = -1e30
SCALE = math.log2(math.e) / math.sqrt(HDIM)
MESH = pl.DeviceIdType.MESH
scope = jax.named_scope


def kernel(
    zs,
    sections,
    stream,
    queries,
    fresh_k,
    fresh_v,
    stale_k,
    stale_v,
    gate,
    patch,
    text,
    att_out,
    next_out,
    q_all,
    k_all,
    v_all,
    part,
    stat,
    got,
    got_stat,
    fin,
    rows_in,
    incoming,
    gate_v,
    patch_s,
    text_s,
    local_sem,
    local_kv,
    stream_sem,
    q_send,
    q_recv,
    kv_send,
    kv_recv,
    zq_send,
    zq_recv,
    p_send,
    p_recv,
    s_send,
    s_recv,
    f_send,
    f_recv,
):
    section = lax.axis_index("section")
    rank = lax.axis_index("seq")
    z = rank // QUAD
    g = rank % QUAD
    stale = stale_k.shape[0]
    rows = queries.shape[0]
    width = queries.shape[1] // QUAD
    block = rows * QUAD
    heads = width // HDIM
    stale_total = stale * QUAD
    after = {"section": (section + 1) % sections}
    before = {"section": (section + sections - 1) % sections}

    def quad_at(k):
        return (g + k) % QUAD

    def quad_peer(k):
        return {"seq": z * QUAD + quad_at(k)}

    def z_peer(d):
        return {"seq": ((z + d + zs) % zs) * QUAD + g}

    barrier = pltpu.get_barrier_semaphore()
    peers = [quad_peer(k) for k in range(1, QUAD)] + [z_peer(d) for d in range(1, zs)] + [after, before]
    for peer in peers:
        pl.semaphore_signal(barrier, inc=1, device_id=peer, device_id_type=MESH)

    def columns(group, head=0, count=width):
        return pl.ds(pl.multiple_of(group * width + head * HDIM, 128), count)

    def quad_rows(group, count, first=0):
        return pl.ds(pl.multiple_of(first + group * count, 16), count)

    sources = (
        (stale_k, k_all, quad_rows(g, stale)),
        (fresh_k, k_all, quad_rows(g, rows, stale_total)),
        (stale_v, v_all, quad_rows(g, stale)),
        (fresh_v, v_all, quad_rows(g, rows, stale_total)),
    )
    small = [
        pltpu.make_async_copy(queries.at[:, columns(g)], q_all.at[0, quad_rows(g, rows)], local_sem.at[0]),
        pltpu.make_async_copy(patch, patch_s, local_sem.at[1]),
        pltpu.make_async_copy(text, text_s, local_sem.at[2]),
        pltpu.make_async_copy(gate, gate_v, local_sem.at[3]),
    ]
    own_kv = [
        [
            pltpu.make_async_copy(src.at[:, columns(g, h, HDIM)], dst.at[h, where], local_kv.at[h, n])
            for n, (src, dst, where) in enumerate(sources)
        ]
        for h in range(heads)
    ]
    for copy in small + sum(own_kv, []):
        copy.start()

    with scope("barrier"):
        pl.semaphore_wait(barrier, len(peers))

    started = []

    def send(src, dst, send_sem, recv_sem, peer):
        copy = pltpu.make_async_remote_copy(
            src_ref=src, dst_ref=dst, send_sem=send_sem, recv_sem=recv_sem, device_id=peer, device_id_type=MESH
        )
        copy.start()
        started.append(copy)
        return copy

    crossing = (2, 3, 1)
    quad_q = [
        send(
            queries.at[:, columns(quad_at(k))],
            q_all.at[0, quad_rows(g, rows)],
            q_send.at[k - 1],
            q_recv.at[k - 1],
            quad_peer(k),
        )
        for k in crossing
    ]
    quad_kv = [
        [
            send(
                src.at[:, columns(quad_at(k), h, HDIM)],
                dst.at[h, where],
                kv_send.at[h, n, k - 1],
                kv_recv.at[h, n, k - 1],
                quad_peer(k),
            )
            for n, (src, dst, where) in enumerate(sources)
            for k in crossing
        ]
        for h in range(heads)
    ]
    stream_copy = send(stream, incoming, stream_sem.at[0], stream_sem.at[1], after)

    with scope("qwait"):
        small[0].wait()
        for copy in quad_q:
            copy.wait_recv()

    arrival = {}

    def pass_on(source, d):
        arrival[d] = [send(q_all.at[source], q_all.at[d], zq_send.at[d], zq_recv.at[d], z_peer(d - source))]

    for d in (2, zs - 2, 1, zs - 1):
        pass_on(0, d)

    with scope("mask"):
        small[1].wait()
        small[2].wait()
        spot = lax.broadcasted_iota(jnp.int32, (1, stale_total + block), 1)
        position = z * stale_total + spot
        region = (position - TXT) // (block * zs)
        floor = jnp.float32(FLOOR_SCORE)
        text_bias = jnp.where(position < text_s[0, 0], 0.0, floor)
        image_bias = jnp.where(region == patch_s[0, 0], floor, 0.0)
        bias = jnp.where(position < TXT, text_bias, image_bias)
        bias = jnp.where(spot < stale_total, bias, 0.0)

    half = block // 2
    with scope("relay"):
        for near, far, turn in ((2, 3, 0), (zs - 2, zs - 3, 1)):
            arrival[near][0].wait_recv()
            pass_on(near, far)
            piece = pl.ds(turn * half, half)
            extra = send(
                q_all.at[near, piece],
                q_all.at[zs // 2, piece],
                zq_send.at[zs // 2 + turn * (zs // 2)],
                zq_recv.at[zs // 2 + turn * (zs // 2)],
                z_peer(near),
            )
            arrival.setdefault(zs // 2, []).append(extra)
    arrival[2], arrival[zs - 2] = [], []
    arrival[0] = []

    lane = lax.broadcasted_iota(jnp.int32, (block, 128), 1)
    partial = [[None] * zs for _ in range(heads)]
    mid = zs // 2
    first_order = [0, 2, zs - 2, 1, zs - 1, 3, zs - 3, mid]
    later_order = [mid, 3, zs - 3, 2, zs - 2, 1, zs - 1, 0]
    for h in range(heads):
        with scope(f"kv#h={h}"):
            for copy in own_kv[h]:
                copy.wait()
            for copy in quad_kv[h]:
                copy.wait_recv()
        cols = slice(h * HDIM, (h + 1) * HDIM)
        stats = jnp.zeros((block, 128), jnp.float32)
        for d in first_order if h == 0 else later_order:
            if h == 0:
                with scope(f"zq#d={d}"):
                    for copy in arrival[d]:
                        copy.wait_recv()
            s = lax.dot_general(
                q_all[d, :, cols], k_all[h], (((1,), (1,)), ((), ())), preferred_element_type=jnp.float32
            )
            s = s * SCALE + bias
            m = jnp.max(s, axis=1, keepdims=True)
            p = jnp.exp2(s - m)
            total = jnp.sum(p, axis=1, keepdims=True)
            o = jnp.dot(p.astype(jnp.bfloat16), v_all[h], preferred_element_type=jnp.float32)
            stats = jnp.where(lane == 2 * d, m, stats)
            stats = jnp.where(lane == 2 * d + 1, total, stats)
            o_ref = part.at[h, d] if d else got.at[h, 0]
            o_ref[...] = o.astype(jnp.bfloat16)
            if d:
                partial[h][d] = send(
                    part.at[h, d], got.at[h, d], p_send.at[h, d], p_recv.at[h, d], z_peer(-d)
                )
        turned = jnp.transpose(stats)
        for d in range(zs):
            s_ref = stat.at[h, d] if d else got_stat.at[h, 0]
            s_ref[:, 0:block] = turned[2 * d : 2 * d + 2, :]
        partial[h] = partial[h][1:] + [
            send(stat.at[h, d], got_stat.at[h, d], s_send.at[h, d], s_recv.at[h, d], z_peer(-d))
            for d in range(1, zs)
        ]

    for h in range(heads):
        with scope(f"pwait#h={h}"):
            for copy in partial[h]:
                copy.wait_recv()
        tops = jnp.concatenate([got_stat[h, d, 0:1, 0:block] for d in range(zs)], axis=0)
        sums = jnp.concatenate([got_stat[h, d, 1:2, 0:block] for d in range(zs)], axis=0)
        factors = jnp.exp2(tops - jnp.max(tops, axis=0, keepdims=True))
        share = factors / jnp.sum(factors * sums, axis=0, keepdims=True)
        pad = jnp.zeros((128 - zs, block), jnp.float32)
        share = jnp.transpose(jnp.concatenate([share, pad], axis=0))
        acc = jnp.zeros((block, HDIM), jnp.float32)
        for d in range(zs):
            acc = acc + share[:, d : d + 1] * got[h, d].astype(jnp.float32)
        fin[:, h * HDIM : (h + 1) * HDIM] = acc.astype(jnp.bfloat16)

    back = [
        send(fin.at[quad_rows(quad_at(k), rows)], rows_in.at[g], f_send.at[k - 1], f_recv.at[k - 1], quad_peer(k))
        for k in crossing
    ]
    rows_in[g] = fin[quad_rows(g, rows), :]
    with scope("owait"):
        small[3].wait()
        stream_copy.wait_recv()
        for copy in back:
            copy.wait_recv()
    for k in range(QUAD):
        cols = slice(k * width, (k + 1) * width)
        att = rows_in[k]
        att_out[:, cols] = att
        next_out[:, cols] = (
            incoming[:, cols].astype(jnp.float32) + gate_v[:, cols] * att.astype(jnp.float32)
        ).astype(jnp.bfloat16)
    with scope("drain"):
        for copy in started:
            copy.wait_send()


def local(mesh_sizes, stream, queries, fresh_keys, fresh_values, stale_keys, stale_values, gate, patch, text):
    sections, seq = mesh_sizes
    zs = seq // QUAD
    rows, channels = queries.shape[1:]
    stale = stale_keys.shape[1]
    width = channels // QUAD
    heads = width // HDIM
    block = rows * QUAD
    keys = (stale + rows) * QUAD
    bf16, f32, i32 = jnp.bfloat16, jnp.float32, jnp.int32
    dma = pltpu.SemaphoreType.DMA
    hbm = pl.BlockSpec(memory_space=pl.ANY)
    vmem = pl.BlockSpec(memory_space=pltpu.VMEM)
    att, nxt = pl.pallas_call(
        functools.partial(kernel, zs, sections),
        out_shape=[pltpu.VMEM((rows, channels), bf16)] * 2,
        in_specs=[hbm] * 9,
        out_specs=[vmem] * 2,
        scratch_shapes=[
            pltpu.VMEM((zs, block, width), bf16),
            pltpu.VMEM((heads, keys, HDIM), bf16),
            pltpu.VMEM((heads, keys, HDIM), bf16),
            pltpu.VMEM((heads, zs, block, HDIM), bf16),
            pltpu.VMEM((heads, zs, 2, 128), f32),
            pltpu.VMEM((heads, zs, block, HDIM), bf16),
            pltpu.VMEM((heads, zs, 2, 128), f32),
            pltpu.VMEM((block, width), bf16),
            pltpu.VMEM((QUAD, rows, width), bf16),
            pltpu.VMEM((rows, channels), bf16),
            pltpu.VMEM((1, channels), f32),
            pltpu.SMEM((1, 1), i32),
            pltpu.SMEM((1, 1), i32),
            dma((4,)),
            dma((heads, 4)),
            dma((2,)),
            dma((3,)),
            dma((3,)),
            dma((heads, 4, 3)),
            dma((heads, 4, 3)),
            dma((zs + 1,)),
            dma((zs + 1,)),
            dma((heads, zs)),
            dma((heads, zs)),
            dma((heads, zs)),
            dma((heads, zs)),
            dma((3,)),
            dma((3,)),
        ],
        compiler_params=pltpu.CompilerParams(
            collective_id=0, has_side_effects=True
        ),
    )(
        stream[0],
        queries[0],
        fresh_keys[0],
        fresh_values[0],
        stale_keys[0],
        stale_values[0],
        gate,
        patch[None],
        text[None],
    )
    return att[None], nxt[None]


def solution(mesh):
    rowed = P("section", "seq", None)
    return jax.shard_map(
        functools.partial(local, (mesh.shape["section"], mesh.shape["seq"])),
        mesh=mesh,
        in_specs=(rowed,) * 6 + (P("section", None), P("section"), P()),
        out_specs=(rowed, rowed),
        check_vma=False,
    )
```

time: 49.8 us -> 44.3 us (0.89)
  Pallas kernels: 45.7 us -> 41.1 us
  local copies, waits for them, and re-layouts: 2.06 us -> 1.24 us
    pallas_call x1, Pallas kernels: 45.7 us -> 41.1 us  [local(): pl.pallas_call(functools.partial(kernel, zs, sections), out_shape=[pltpu....]
    unnamed x4 -> x2, local copies, waits for them, and re-layouts: 2.06 us -> 1.24 us
where the time goes in v2:
time: 44.3 us; the launch traced here: 44.2 us
  Pallas kernels  41.1 us (93%)
  between operations  1.93 us (4%)
  local copies, waits for them, and re-layouts  1.24 us (3%)
    pallas_call x1, Pallas kernels, local(): pl.pallas_call(functools.partial(kernel, zs, sections), out_shape=[pltpu....  41.1 us
    unnamed x2, local copies, waits for them, and re-layouts  1.24 us

profile of v2, /device:TPU:1, one launch (start us, length us, event | category | flops | bytes accessed | tf_op | source)
XLA Modules:
  0.0 44.2 jit_solution(10364658173731194020)
XLA Ops:
  1.9 41.1 %shard_map.104 = (bf16[16,1536]{1,0:T(8,128)(2,1)S(1)}, bf16[16,1536]{1,0:T(8,128)(2,1)S(1)}) custom-call(bf16[16,1536]{1,0:T(8,128)(2,1)} %bitcast.16, bf16[16,1536]{1,0:T(8,128)(2,1)} %bitcast.17, bf16[16,1536]{1,0:T(8,128)(2,1)} %bitcast.18, bf16[16,1536]{1,0:T(8,128)(2,1)} %bitcast.19, bf16[144,1536]{1,0:T(8,128)(2,1)} %bitcast.14, ...), custom_call_target="tpu_custom_call" | custom-call | tf_op jit(solution)/shard_map/pallas_call | solution.py:293
  43.0 0.6 %copy.13 = bf16[1,16,1536]{2,1,0:T(8,128)(2,1)} copy(bf16[1,16,1536]{2,1,0:T(8,128)(2,1)S(1)} %bitcast.13) | data formatting | bytes 98304
  43.6 0.6 %copy.14 = bf16[1,16,1536]{2,1,0:T(8,128)(2,1)} copy(bf16[1,16,1536]{2,1,0:T(8,128)(2,1)S(1)} %bitcast.12) | data formatting | bytes 98304

commit v3 on v2

--- a/solution.py
+++ b/solution.py
@@ -44,6 +44,11 @@
     gate_v,
     patch_s,
     text_s,
+    q_held,
+    sk_held,
+    fk_held,
+    sv_held,
+    fv_held,
     local_sem,
     local_kv,
     stream_sem,
@@ -83,15 +88,34 @@
         return {"seq": ((z + d + zs) % zs) * QUAD + g}
 
     barrier = pltpu.get_barrier_semaphore()
-    peers = [quad_peer(k) for k in range(1, QUAD)] + [z_peer(d) for d in range(1, zs)] + [after, before]
+    peers = [quad_peer(k) for k in range(1, QUAD)] + [z_peer(d) for d in range(1, zs)]
+    first = section == 0
+
+    def greet(peer):
+        pl.semaphore_signal(barrier, inc=1, device_id=peer, device_id_type=MESH)
+
     for peer in peers:
-        pl.semaphore_signal(barrier, inc=1, device_id=peer, device_id_type=MESH)
+        greet(peer)
+
+    @pl.when(section > 1)
+    def _():
+        greet(before)
+
+    @pl.when(jnp.logical_and(section > 0, section < sections - 1))
+    def _():
+        greet(after)
 
     def columns(group, head=0, count=width):
         return pl.ds(pl.multiple_of(group * width + head * HDIM, 128), count)
 
     def quad_rows(group, count, first=0):
         return pl.ds(pl.multiple_of(first + group * count, 16), count)
+
+    chunk = zs // 2
+    order = [0, 1, zs - 1, zs - 2, 2, zs - 3, 3, zs // 2]
+
+    def slot(d, first=0, count=block):
+        return pl.ds(pl.multiple_of(order.index(d) * block + first, 16), count)
 
     sources = (
         (stale_k, k_all, quad_rows(g, stale)),
@@ -100,11 +124,19 @@
         (fresh_v, v_all, quad_rows(g, rows, stale_total)),
     )
     small = [
-        pltpu.make_async_copy(queries.at[:, columns(g)], q_all.at[0, quad_rows(g, rows)], local_sem.at[0]),
+        pltpu.make_async_copy(queries.at[:, columns(g)], q_all.at[slot(0, g * rows, rows)], local_sem.at[0]),
         pltpu.make_async_copy(patch, patch_s, local_sem.at[1]),
         pltpu.make_async_copy(text, text_s, local_sem.at[2]),
         pltpu.make_async_copy(gate, gate_v, local_sem.at[3]),
     ]
+    arrays = (stale_k, fresh_k, stale_v, fresh_v)
+    staged = [pltpu.make_async_copy(queries, q_held, local_sem.at[4])]
+    staged += [
+        pltpu.make_async_copy(src, dst, local_sem.at[5 + n])
+        for n, (src, dst) in enumerate(zip(arrays, (sk_held, fk_held, sv_held, fv_held)))
+    ]
+    for copy in staged:
+        copy.start()
     own_kv = [
         [
             pltpu.make_async_copy(src.at[:, columns(g, h, HDIM)], dst.at[h, where], local_kv.at[h, n])
@@ -116,7 +148,24 @@
         copy.start()
 
     with scope("barrier"):
-        pl.semaphore_wait(barrier, len(peers))
+
+        @pl.when(first)
+        def _():
+            pl.semaphore_wait(barrier, len(peers))
+            greet(after)
+            greet(before)
+
+        @pl.when(jnp.logical_not(first))
+        def _():
+            pl.semaphore_wait(barrier, len(peers) + 2)
+
+        @pl.when(section == 1)
+        def _():
+            greet(before)
+
+        @pl.when(section == sections - 1)
+        def _():
+            greet(after)
 
     started = []
 
@@ -129,10 +178,12 @@
         return copy
 
     crossing = (2, 3, 1)
+    for copy in staged:
+        copy.wait()
     quad_q = [
         send(
-            queries.at[:, columns(quad_at(k))],
-            q_all.at[0, quad_rows(g, rows)],
+            q_held.at[:, columns(quad_at(k))],
+            q_all.at[slot(0, g * rows, rows)],
             q_send.at[k - 1],
             q_recv.at[k - 1],
             quad_peer(k),
@@ -142,18 +193,17 @@
     quad_kv = [
         [
             send(
-                src.at[:, columns(quad_at(k), h, HDIM)],
+                held.at[:, columns(quad_at(k), h, HDIM)],
                 dst.at[h, where],
                 kv_send.at[h, n, k - 1],
                 kv_recv.at[h, n, k - 1],
                 quad_peer(k),
             )
-            for n, (src, dst, where) in enumerate(sources)
+            for n, (held, (_, dst, where)) in enumerate(zip((sk_held, fk_held, sv_held, fv_held), sources))
             for k in crossing
         ]
         for h in range(heads)
     ]
-    stream_copy = send(stream, incoming, stream_sem.at[0], stream_sem.at[1], after)
 
     with scope("qwait"):
         small[0].wait()
@@ -163,7 +213,7 @@
     arrival = {}
 
     def pass_on(source, d):
-        arrival[d] = [send(q_all.at[source], q_all.at[d], zq_send.at[d], zq_recv.at[d], z_peer(d - source))]
+        arrival[d] = [send(q_all.at[slot(source)], q_all.at[slot(d)], zq_send.at[d], zq_recv.at[d], z_peer(d - source))]
 
     for d in (2, zs - 2, 1, zs - 1):
         pass_on(0, d)
@@ -185,10 +235,9 @@
         for near, far, turn in ((2, 3, 0), (zs - 2, zs - 3, 1)):
             arrival[near][0].wait_recv()
             pass_on(near, far)
-            piece = pl.ds(turn * half, half)
             extra = send(
-                q_all.at[near, piece],
-                q_all.at[zs // 2, piece],
+                q_all.at[slot(near, turn * half, half)],
+                q_all.at[slot(zs // 2, turn * half, half)],
                 zq_send.at[zs // 2 + turn * (zs // 2)],
                 zq_recv.at[zs // 2 + turn * (zs // 2)],
                 z_peer(near),
@@ -197,11 +246,17 @@
     arrival[2], arrival[zs - 2] = [], []
     arrival[0] = []
 
-    lane = lax.broadcasted_iota(jnp.int32, (block, 128), 1)
-    partial = [[None] * zs for _ in range(heads)]
-    mid = zs // 2
-    first_order = [0, 2, zs - 2, 1, zs - 1, 3, zs - 3, mid]
-    later_order = [mid, 3, zs - 3, 2, zs - 2, 1, zs - 1, 0]
+    with scope("greeted"):
+
+        @pl.when(first)
+        def _():
+            pl.semaphore_wait(barrier, 2)
+
+    stream_copy = send(stream, incoming, stream_sem.at[0], stream_sem.at[1], after)
+
+    lane = lax.broadcasted_iota(jnp.int32, (chunk * block, 128), 1)
+    partial = [[] for _ in range(heads)]
+    early, late = list(range(chunk)), list(range(chunk, zs))
     for h in range(heads):
         with scope(f"kv#h={h}"):
             for copy in own_kv[h]:
@@ -209,36 +264,38 @@
             for copy in quad_kv[h]:
                 copy.wait_recv()
         cols = slice(h * HDIM, (h + 1) * HDIM)
-        stats = jnp.zeros((block, 128), jnp.float32)
-        for d in first_order if h == 0 else later_order:
+        for slots in (early, late) if h == 0 else (late, early):
             if h == 0:
-                with scope(f"zq#d={d}"):
-                    for copy in arrival[d]:
-                        copy.wait_recv()
+                with scope(f"zq#n={slots[0]}"):
+                    for n in slots:
+                        for copy in arrival[order[n]]:
+                            copy.wait_recv()
             s = lax.dot_general(
-                q_all[d, :, cols], k_all[h], (((1,), (1,)), ((), ())), preferred_element_type=jnp.float32
+                q_all[slots[0] * block : slots[0] * block + chunk * block, cols],
+                k_all[h],
+                (((1,), (1,)), ((), ())),
+                preferred_element_type=jnp.float32,
             )
             s = s * SCALE + bias
             m = jnp.max(s, axis=1, keepdims=True)
             p = jnp.exp2(s - m)
             total = jnp.sum(p, axis=1, keepdims=True)
             o = jnp.dot(p.astype(jnp.bfloat16), v_all[h], preferred_element_type=jnp.float32)
-            stats = jnp.where(lane == 2 * d, m, stats)
-            stats = jnp.where(lane == 2 * d + 1, total, stats)
-            o_ref = part.at[h, d] if d else got.at[h, 0]
-            o_ref[...] = o.astype(jnp.bfloat16)
-            if d:
-                partial[h][d] = send(
-                    part.at[h, d], got.at[h, d], p_send.at[h, d], p_recv.at[h, d], z_peer(-d)
-                )
-        turned = jnp.transpose(stats)
-        for d in range(zs):
-            s_ref = stat.at[h, d] if d else got_stat.at[h, 0]
-            s_ref[:, 0:block] = turned[2 * d : 2 * d + 2, :]
-        partial[h] = partial[h][1:] + [
-            send(stat.at[h, d], got_stat.at[h, d], s_send.at[h, d], s_recv.at[h, d], z_peer(-d))
-            for d in range(1, zs)
-        ]
+            o = o.astype(jnp.bfloat16)
+            turned = jnp.transpose(jnp.where(lane == 0, m, total))
+            for n in slots if h == 0 else slots[::-1]:
+                d = order[n]
+                at = slice((n - slots[0]) * block, (n - slots[0] + 1) * block)
+                o_ref, s_ref = (part.at[h, d], stat.at[h, d]) if d else (got.at[h, 0], got_stat.at[h, 0])
+                o_ref[...] = o[at]
+                s_ref[:, 0:block] = turned[0:2, at]
+                if d:
+                    partial[h].append(
+                        send(part.at[h, d], got.at[h, d], p_send.at[h, d], p_recv.at[h, d], z_peer(-d))
+                    )
+                    partial[h].append(
+                        send(stat.at[h, d], got_stat.at[h, d], s_send.at[h, d], s_recv.at[h, d], z_peer(-d))
+                    )
 
     for h in range(heads):
         with scope(f"pwait#h={h}"):
@@ -296,7 +353,7 @@
         in_specs=[hbm] * 9,
         out_specs=[vmem] * 2,
         scratch_shapes=[
-            pltpu.VMEM((zs, block, width), bf16),
+            pltpu.VMEM((zs * block, width), bf16),
             pltpu.VMEM((heads, keys, HDIM), bf16),
             pltpu.VMEM((heads, keys, HDIM), bf16),
             pltpu.VMEM((heads, zs, block, HDIM), bf16),
@@ -309,7 +366,12 @@
             pltpu.VMEM((1, channels), f32),
             pltpu.SMEM((1, 1), i32),
             pltpu.SMEM((1, 1), i32),
-            dma((4,)),
+            pltpu.VMEM((rows, channels), bf16),
+            pltpu.VMEM((stale, channels), bf16),
+            pltpu.VMEM((rows, channels), bf16),
+            pltpu.VMEM((stale, channels), bf16),
+            pltpu.VMEM((rows, channels), bf16),
+            dma((9,)),
             dma((heads, 4)),
             dma((2,)),
             dma((3,)),

time: 44.3 us -> 39.6 us (0.89); the launches traced: 44.2 us -> 38.9 us
  Pallas kernels: 41.1 us -> 35.7 us
    pallas_call x1, Pallas kernels: 41.1 us -> 35.7 us  [local(): pl.pallas_call(functools.partial(kernel, zs, sections), out_shape=[pltpu....]
where the time goes in v3:
time: 39.6 us; the launch traced here: 38.9 us
  Pallas kernels  35.7 us (90%)
  between operations  1.93 us (5%)
  local copies, waits for them, and re-layouts  1.24 us (3%)
    pallas_call x1, Pallas kernels, local(): pl.pallas_call(functools.partial(kernel, zs, sections), out_shape=[pltpu....  35.7 us
    unnamed x2, local copies, waits for them, and re-layouts  1.24 us

profile of v3, /device:TPU:1, one launch (start us, length us, event | category | flops | bytes accessed | tf_op | source)
XLA Modules:
  0.0 38.9 jit_solution(2883226907124073384)
XLA Ops:
  1.9 35.7 %shard_map.104 = (bf16[16,1536]{1,0:T(8,128)(2,1)S(1)}, bf16[16,1536]{1,0:T(8,128)(2,1)S(1)}) custom-call(bf16[16,1536]{1,0:T(8,128)(2,1)} %bitcast.16, bf16[16,1536]{1,0:T(8,128)(2,1)} %bitcast.17, bf16[16,1536]{1,0:T(8,128)(2,1)} %bitcast.18, bf16[16,1536]{1,0:T(8,128)(2,1)} %bitcast.19, bf16[144,1536]{1,0:T(8,128)(2,1)} %bitcast.14, ...), custom_call_target="tpu_custom_call" | custom-call | tf_op jit(solution)/shard_map/pallas_call | solution.py:350
  37.7 0.6 %copy.13 = bf16[1,16,1536]{2,1,0:T(8,128)(2,1)} copy(bf16[1,16,1536]{2,1,0:T(8,128)(2,1)S(1)} %bitcast.13) | data formatting | bytes 98304
  38.3 0.6 %copy.14 = bf16[1,16,1536]{2,1,0:T(8,128)(2,1)} copy(bf16[1,16,1536]{2,1,0:T(8,128)(2,1)S(1)} %bitcast.12) | data formatting | bytes 98304
